TPU v7x, 128 devices: a whole 4x4x4 slice. The times are simulated.
128 devices in a mesh: node: 8 (over z, core), local: 16 (over y, x).
Axes of the slice: x: 4, y: 4, z: 4, core: 2. Of those that a mesh axis runs over, the one named last changes fastest.
Arguments:
- tokens: bfloat16 [2048, 7168], P(('node', 'local')), may hold values from -6 to 6
- grad_out: bfloat16 [2048, 7168], P(('node', 'local')), may hold values from -6 to 6
- gates: bfloat16 [2048, 3], P(('node', 'local')), may hold values from 0.19921875 to 1
- expert_ids: int32 [2048, 3], P(('node', 'local')), may hold values from 0 to 15, as said below
- w_gate: bfloat16 [8, 7168, 2048], P('node', None, 'local'), may hold values from -0.0625 to 0.0625
- w_up: bfloat16 [8, 7168, 2048], P('node', None, 'local'), may hold values from -0.0625 to 0.0625
- w_down: bfloat16 [8, 7168, 2048], P('node', None, 'local'), may hold values from -0.1875 to 0.1875
- s_gate: bfloat16 [7168, 2048], P(None, 'local'), may hold values from -0.0625 to 0.0625
- s_up: bfloat16 [7168, 2048], P(None, 'local'), may hold values from -0.0625 to 0.0625
- s_down: bfloat16 [7168, 2048], P(None, 'local'), may hold values from -0.125 to 0.125
Outputs:
- dx: bfloat16 [2048, 7168], P(('node', 'local'))
- dgates: float32 [2048, 3], P(('node', 'local'))
- d_w_gate: bfloat16 [8, 7168, 2048], P('node', None, 'local')
- d_w_up: bfloat16 [8, 7168, 2048], P('node', None, 'local')
- d_w_down: bfloat16 [8, 7168, 2048], P('node', None, 'local')
- d_s_gate: bfloat16 [7168, 2048], P('node', 'local')
- d_s_up: bfloat16 [7168, 2048], P('node', 'local')
- d_s_down: bfloat16 [7168, 2048], P('node', 'local')
Inputs may be any that keep to these rules, and one draw needn't show every extreme that they name: `expert_ids`: each token names both experts of one node and one expert of a second node. Of the tokens of one device exactly 4 name experts of each node and at most 4 name any one expert; for every node one of its experts is named by exactly 4 tokens of every device.
All inputs are finite; a program needn't handle non-finite values.
Results may differ from a plain program's by a relative error of at most 0.014.
Values may be sent and summed in bfloat16 or wider, within the bound.
No kernel may reach another device: no remote copies, remote signals or barrier semaphores. Data moves between devices by JAX's collectives and lax.ppermute only.
A program may use at most 192 MiB of HBM per device.

v0:
```python
import jax
import jax.numpy as jnp
from jax import lax
from jax.sharding import PartitionSpec as P

E_NODE = 2
precise = lax.Precision.HIGHEST


def split_up(value, dim, devices):
    before, after = (value.shape[:dim], value.shape[dim + 1 :])
    return jnp.moveaxis(value.reshape(*before, devices, -1, *after), dim, 0)


def summed_on_arrival(value, axis, dim):
    tiles = split_up(value, dim, lax.axis_size(axis))
    arrived = lax.all_to_all(tiles, axis, split_axis=0, concat_axis=0, tiled=True)
    return arrived.astype(jnp.float32).sum(axis=0)


def in_one_piece(arrays, axis, split_dim, concat_dim, along):
    columns = [a.reshape(*a.shape[:along], -1) for a in arrays]
    both = jnp.concatenate(columns, axis=along)
    out, at, gathered = (
        lax.all_to_all(both, axis, split_axis=split_dim, concat_axis=concat_dim, tiled=True),
        0,
        [],
    )
    for a, column in zip(arrays, columns):
        piece = out[..., at : at + column.shape[along]]
        gathered.append(piece.reshape(*piece.shape[:along], *a.shape[along:]))
        at += column.shape[along]
    return tuple(gathered)


def silu_parts(pre_gate):
    sig = jax.nn.sigmoid(pre_gate)
    return (pre_gate * sig, sig * (1.0 + pre_gate * (1.0 - sig)))


def contract_first(left, right):
    return lax.dot_general(
        left, right, (((0,), (0,)), ((), ())), preferred_element_type=jnp.float32
    )


def contract_last(left, right):
    return lax.dot_general(
        left, right, (((1,), (1,)), ((), ())), preferred_element_type=jnp.float32
    )


def ffn_backward(rows_in, rows_grad, weight, gate_w, up_w, down_w):
    pre_gate = jnp.dot(rows_in, gate_w, preferred_element_type=jnp.float32)
    pre_up = jnp.dot(rows_in, up_w, preferred_element_type=jnp.float32)
    activ, slope = silu_parts(pre_gate)
    hidden = activ * pre_up
    upstream = jnp.dot(rows_grad, down_w, preferred_element_type=jnp.float32)
    scaled = weight * upstream
    grad_up = (scaled * activ).astype(jnp.bfloat16)
    grad_gate = (scaled * pre_up * slope).astype(jnp.bfloat16)
    weighted = (weight * hidden).astype(jnp.bfloat16)
    return (grad_gate, grad_up, weighted, hidden * upstream)


def expert_work(rows_in, rows_grad, weight, gate_w, up_w, down_w):
    grad_gate, grad_up, weighted, product = ffn_backward(
        rows_in, rows_grad, weight, gate_w, up_w, down_w
    )
    partial_value = (contract_last(grad_gate, gate_w) + contract_last(grad_up, up_w)).astype(
        jnp.bfloat16
    )
    score = jnp.sum(product, axis=1).astype(jnp.bfloat16)
    grads = (
        contract_first(rows_in, grad_gate),
        contract_first(rows_in, grad_up),
        contract_first(rows_grad, weighted),
    )
    return (partial_value, score, grads)


def shared_part(tokens, grad_out, s_gate, s_up, s_down):
    rows_in, rows_grad = (
        lax.all_gather(tokens, "local", axis=0, tiled=True),
        lax.all_gather(grad_out, "local", axis=0, tiled=True),
    )
    unit_weight = jnp.ones((rows_in.shape[0], 1), jnp.float32)
    grad_gate, grad_up, weighted, product = ffn_backward(
        rows_in, rows_grad, unit_weight, s_gate, s_up, s_down
    )
    dx_shared = summed_on_arrival(
        (contract_last(grad_gate, s_gate) + contract_last(grad_up, s_up)).astype(jnp.bfloat16),
        "local",
        0,
    )
    units = s_gate.shape[1]
    shares = lax.psum_scatter(
        jnp.concatenate(
            [
                contract_first(rows_in, grad_gate),
                contract_first(rows_in, grad_up),
                contract_first(rows_grad, weighted),
            ],
            axis=1,
        ).astype(jnp.bfloat16),
        "node",
        scatter_dimension=0,
        tiled=True,
    ).astype(jnp.float32)
    shared_grads = (
        shares[:, :units].astype(jnp.bfloat16),
        shares[:, units : 2 * units].astype(jnp.bfloat16),
        shares[:, 2 * units :].astype(jnp.bfloat16),
    )
    return (dx_shared, shared_grads)


def routed_part(tokens, grad_out, gates, expert_ids, gate_w, up_w, down_w):
    tokens_here = tokens.shape[0]
    width = tokens.shape[1]
    node_count = lax.axis_size("node")
    local_count = lax.axis_size("local")
    group_size = local_count // E_NODE
    capacity = 2 * tokens_here // node_count
    expert_count = E_NODE * node_count
    slots = jnp.arange(capacity, dtype=jnp.int32)
    chosen = expert_ids[:, :, None] == jnp.arange(expert_count, dtype=jnp.int32)[None, None, :]
    member = jnp.any(chosen, axis=1)
    weight = jnp.sum(jnp.where(chosen, gates.astype(jnp.float32)[:, :, None], 0.0), axis=1)
    ranking = jnp.cumsum(member.astype(jnp.int32), axis=0) - 1
    slot_pick = member[:, :, None] & (ranking[:, :, None] == slots[None, None, :])
    pick_float = slot_pick.astype(jnp.float32)
    slot_gate = jnp.einsum("tes,te->es", pick_float, weight, precision=precise)
    pick_rows = slot_pick.astype(jnp.bfloat16)
    send_in = jnp.einsum(
        "tes,td->esd", pick_rows, tokens, preferred_element_type=jnp.float32
    ).astype(jnp.bfloat16)
    send_grad = jnp.einsum(
        "tes,td->esd", pick_rows, grad_out, preferred_element_type=jnp.float32
    ).astype(jnp.bfloat16)

    def spread(values):
        shaped = values.reshape((node_count, E_NODE, 1) + values.shape[1:])
        wide = jnp.broadcast_to(shaped, (node_count, E_NODE, group_size) + values.shape[1:])
        return wide.reshape((node_count * local_count,) + values.shape[1:])

    got_in, got_grad, got_gate = in_one_piece(
        (spread(send_in), spread(send_grad), spread(slot_gate.astype(jnp.bfloat16))),
        ("node", "local"),
        0,
        0,
        2,
    )
    partial_value, score, grads = expert_work(
        got_in.reshape(-1, width),
        got_grad.reshape(-1, width),
        got_gate.reshape(-1, 1).astype(jnp.float32),
        gate_w,
        up_w,
        down_w,
    )
    back_dx, back_score = (
        lax.all_to_all(
            partial_value.reshape(got_in.shape),
            ("node", "local"),
            split_axis=0,
            concat_axis=0,
            tiled=True,
        ),
        lax.all_to_all(
            score.reshape(got_gate.shape),
            ("node", "local"),
            split_axis=0,
            concat_axis=0,
            tiled=True,
        ),
    )
    slot_dx = jnp.sum(
        back_dx.reshape(node_count, E_NODE, group_size, capacity, width).astype(jnp.float32), axis=2
    ).reshape(expert_count, capacity, width)
    slot_score = jnp.sum(
        back_score.reshape(node_count, E_NODE, group_size, capacity).astype(jnp.float32), axis=2
    ).reshape(expert_count, capacity)
    dx_routed = jnp.einsum("tes,esd->td", pick_float, slot_dx, precision=precise)
    token_score = jnp.einsum("tes,es->te", pick_float, slot_score, precision=precise)
    dgates = jnp.sum(jnp.where(chosen, token_score[:, None, :], 0.0), axis=2)
    return (dx_routed, dgates, grads)


def local(tokens, grad_out, gates, expert_ids, w_gate, w_up, w_down, s_gate, s_up, s_down):
    dx_routed, dgates, grads = routed_part(
        tokens, grad_out, gates, expert_ids, w_gate[0], w_up[0], w_down[0]
    )
    dx_shared, shared_grads = shared_part(tokens, grad_out, s_gate, s_up, s_down)
    dx = (dx_routed + dx_shared).astype(jnp.bfloat16)
    expert_grads = tuple((grad.astype(jnp.bfloat16)[None] for grad in grads))
    return (
        dx,
        dgates,
        expert_grads[0],
        expert_grads[1],
        expert_grads[2],
        shared_grads[0],
        shared_grads[1],
        shared_grads[2],
    )


def solution(mesh):
    placed = (
        P(("node", "local"), None),
        P(("node", "local"), None),
        P(("node", "local"), None),
        P(("node", "local"), None),
        P("node", None, "local"),
        P("node", None, "local"),
        P("node", None, "local"),
        P(None, "local"),
        P(None, "local"),
        P(None, "local"),
    )
    return jax.shard_map(
        local,
        mesh=mesh,
        in_specs=placed,
        out_specs=(
            P(("node", "local"), None),
            P(("node", "local"), None),
            P("node", None, "local"),
            P("node", None, "local"),
            P("node", None, "local"),
            P("node", "local"),
            P("node", "local"),
            P("node", "local"),
        ),
        check_vma=False,
    )
```

profile of v0, /device:TPU:11, one launch (start us, length us, event | category | flops | bytes accessed | tf_op | source)
XLA Modules:
  0.0 510.7 jit_solution(10965011893710607387)
XLA Ops:
  7.2 0.0 all-gather.5.cloned.1.call-start
  7.2 0.7 all-gather.5.cloned.1.call-update
  7.9 0.8 fusion.31
  8.7 0.7 convert_element_type.108
  9.4 0.8 select_reduce_fusion.3
  10.2 0.1 copy.81
  10.3 0.1 copy.66
  10.5 0.1 broadcast_in_dim.66
  10.6 0.1 reshape_reshape.4
  10.7 0.2 copy.67
  10.9 1.4 convolution_convert_fusion.6
  12.2 0.7 copy.89
  13.0 1.4 convolution_convert_fusion.7
  14.3 0.7 copy.88
  15.1 5.2 %broadcast_in_dim.60 = bf16[8,2,8,4,7168]{4,3,2,1,0:T(4,128)(2,1)} broadcast(bf16[8,2,4,7168]{3,2,1,0:T(4,128)(2,1)S(1)} %bitcast.98), dimensions={0,1,3,4} | broadcast | bytes 8257536 | tf_op jit(solution)/shard_map/broadcast_in_dim | solution.py:144
  20.3 5.2 %broadcast_in_dim.62 = bf16[8,2,8,4,7168]{4,3,2,1,0:T(4,128)(2,1)} broadcast(bf16[8,2,4,7168]{3,2,1,0:T(4,128)(2,1)S(1)} %bitcast.97), dimensions={0,1,3,4} | broadcast | bytes 8257536 | tf_op jit(solution)/shard_map/broadcast_in_dim | solution.py:144
  25.5 11.0 %pad_maximum_fusion = bf16[128,4,14337]{2,1,0:T(4,128)(2,1)} fusion(bf16[128,4,1]{2,1,0:T(4,128)(2,1)S(1)} %copy.67, bf16[128,4,7168]{2,1,0:T(4,128)(2,1)} %bitcast.94, bf16[128,4,7168]{2,1,0:T(4,128)(2,1)} %bitcast.93), kind=kLoop, calls=%fused_computation | loop fusion | flops 44043264 | bytes 29362176 | tf_op jit(solution)/shard_map/concatenate | solution.py:23
  36.5 11.2 %all-to-all-start = ((bf16[128,4,14337]{2,1,0:T(4,128)(2,1)}), bf16[128,4,14337]{2,1,0:T(4,128)(2,1)}, u32[]{:S(2)}, u32[]{:S(2)}) async-start(bf16[128,4,14337]{2,1,0:T(4,128)(2,1)} %pad_maximum_fusion), calls=%async_computation | async-start | bytes 29622272 | tf_op jit(solution)/shard_map/all_to_all | solution.py:25
  47.7 0.0 all-gather.3.cloned.1.call-start
  47.7 0.7 all-gather.3.cloned.1.call-update
  48.4 0.5 reduce-scatter.4.cloned.1.call-start
  48.9 75.6 %all-gather.5.cloned.1.call-done = bf16[256,7168]{1,0:T(8,128)(2,1)} async-done(((bf16[16,7168]{1,0:T(8,128)(2,1)}), bf16[256,7168]{1,0:T(8,128)(2,1)}) %all-gather.5.cloned.1.call-update) | async-done | bytes 3670032 | tf_op jit(solution)/shard_map/all_gather | solution.py:84
  124.6 3.9 fusion.44
  128.5 0.4 copy-done.6
  128.8 1.2 fusion.43
  130.0 120.8 %all-gather.3.cloned.1.call-done = bf16[256,7168]{1,0:T(8,128)(2,1)} async-done(((bf16[16,7168]{1,0:T(8,128)(2,1)}), bf16[256,7168]{1,0:T(8,128)(2,1)}) %all-gather.3.cloned.1.call-update) | async-done | bytes 3670032 | tf_op jit(solution)/shard_map/all_gather | solution.py:85
  250.8 3.9 multiply_convert_fusion.5
  254.7 0.7 fusion.5
  255.3 0.7 fusion.4
  256.0 1.3 copy-done.8
  257.4 0.7 fusion.6
  258.1 3.1 pad_maximum_fusion.1
  261.2 8.3 %copy.90 = bf16[7168,384]{1,0:T(8,128)(2,1)} copy(bf16[7168,384]{0,1:T(8,128)(2,1)} %pad_maximum_fusion.1) | data formatting | bytes 11010048
  269.5 2.7 fusion.45
  272.3 3.0 fusion
  275.2 11.3 %all-to-all-done = bf16[128,4,14337]{2,1,0:T(4,128)(2,1)} async-done(((bf16[128,4,14337]{2,1,0:T(4,128)(2,1)}), bf16[128,4,14337]{2,1,0:T(4,128)(2,1)}, u32[]{:S(2)}, u32[]{:S(2)}) %all-to-all-start) | async-done | bytes 14681120 | tf_op jit(solution)/shard_map/all_to_all | solution.py:25
  286.5 8.8 %all-to-all-start.2 = ((bf16[16,16,7168]{2,1,0:T(8,128)(2,1)}), bf16[16,16,7168]{2,1,0:T(8,128)(2,1)}, u32[]{:S(2)}, u32[]{:S(2)}) async-start(bf16[16,16,7168]{2,1,0:T(8,128)(2,1)} %bitcast.95), calls=%async_computation.2 | async-start | bytes 7340032 | tf_op jit(solution)/shard_map/all_to_all | solution.py:17
  295.3 15.1 %fusion.41 = (bf16[128,4,7168]{2,1,0:T(4,128)(2,1)}, bf16[128,4,7168]{2,1,0:T(4,128)(2,1)}) fusion(bf16[128,4,14337]{2,1,0:T(4,128)(2,1)} %all-to-all-done), kind=kLoop, calls=%fused_computation.68 | loop fusion | bytes 29360128 | tf_op jit(solution)/shard_map/slice | solution.py:30
  310.4 1.1 convert_reduce_fusion.2
  311.6 0.1 reshape.98
  311.7 12.2 %reshape.92 = bf16[512,7168]{1,0:T(8,128)(2,1)} reshape(bf16[128,4,7168]{2,1,0:T(4,128)(2,1)} %get-tuple-element.48) | data formatting | bytes 14680064 | tf_op jit(solution)/shard_map/reshape | solution.py:156
  323.8 12.1 %reshape.93 = bf16[512,7168]{1,0:T(8,128)(2,1)} reshape(bf16[128,4,7168]{2,1,0:T(4,128)(2,1)} %get-tuple-element.49) | data formatting | bytes 14680064 | tf_op jit(solution)/shard_map/reshape | solution.py:155
  336.0 5.8 %fusion.11 = f32[512,128]{0,1:T(8,128)S(1)} fusion(bf16[512,7168]{1,0:T(8,128)(2,1)} %reshape.93, bf16[1,7168,128]{2,1,0:T(8,128)(2,1)S(1)} %copy-done), kind=kOutput, calls=%fused_computation.26 | convolution fusion | flops 939524096 | bytes 9437184 | tf_op jit(solution)/shard_map/dot_general | solution.py:54
  341.8 2.5 fusion.14
  344.3 0.5 copy-done.2
  344.9 0.5 copy-done.9
  345.4 2.6 multiply_reduce_fusion
  348.0 0.8 convert_element_type.134
  348.7 7.3 %fusion.9 = f32[512,7168]{1,0:T(8,128)} fusion(bf16[512,128]{0,1:T(8,128)(2,1)S(1)} %get-tuple-element.51, bf16[1,7168,128]{2,1,0:T(8,128)(2,1)S(1)} %copy-done), kind=kOutput, calls=%fused_computation.24 | convolution fusion | flops 939524096 | bytes 16646144 | tf_op jit(solution)/shard_map/dot_general | solution.py:48
  356.0 15.4 %all-to-all-start.3 = ((bf16[128,1,4]{2,1,0:T(2,128)(2,1)}), bf16[128,1,4]{2,1,0:T(2,128)(2,1)S(1)}, u32[]{:S(2)}, u32[]{:S(2)}) async-start(bf16[128,1,4]{2,1,0:T(2,128)(2,1)} %convert_element_type.134), calls=%async_computation.3 | async-start | bytes 131072 | tf_op jit(solution)/shard_map/all_to_all | solution.py:170
  371.5 10.7 %add_convert_fusion = bf16[512,7168]{1,0:T(8,128)(2,1)} fusion(f32[512,7168]{1,0:T(8,128)} %fusion.9, bf16[512,128]{0,1:T(8,128)(2,1)S(1)} %get-tuple-element.55, bf16[1,7168,128]{2,1,0:T(8,128)(2,1)} %param.15), kind=kOutput, calls=%fused_computation.2 | convolution fusion | flops 946864128 | bytes 23986176 | tf_op jit(solution)/shard_map/dot_general | solution.py:48
  382.2 12.7 %reshape.94 = bf16[128,4,7168]{2,1,0:T(4,128)(2,1)} reshape(bf16[512,7168]{1,0:T(8,128)(2,1)} %add_convert_fusion) | data formatting | bytes 14680064 | tf_op jit(solution)/shard_map/reshape | solution.py:164
  394.9 10.4 %all-to-all-start.1 = ((bf16[128,4,7168]{2,1,0:T(4,128)(2,1)}), bf16[128,4,7168]{2,1,0:T(4,128)(2,1)}, u32[]{:S(2)}, u32[]{:S(2)}) async-start(bf16[128,4,7168]{2,1,0:T(4,128)(2,1)} %reshape.94), calls=%async_computation.1 | async-start | bytes 14680064 | tf_op jit(solution)/shard_map/all_to_all | solution.py:163
  405.3 2.7 convert_reduce_fusion.1
  408.0 6.6 %fusion.1 = bf16[1,7168,128]{2,1,0:T(8,128)(2,1)} fusion(bf16[512,7168]{1,0:T(8,128)(2,1)} %reshape.93, bf16[512,128]{0,1:T(8,128)(2,1)S(1)} %get-tuple-element.51), kind=kOutput, calls=%fused_computation.11 | convolution fusion | flops 940441600 | bytes 9306112 | tf_op jit(solution)/shard_map/dot_general | solution.py:42
  414.7 3.4 fusion.2
  418.0 3.4 fusion.3
  421.5 0.1 convert_element_type.133
  421.6 0.1 copy.96
  421.7 0.7 select_reduce_fusion.2
  422.4 2.0 fusion.42
  424.4 70.0 %all-to-all-done.1 = bf16[128,4,7168]{2,1,0:T(4,128)(2,1)} async-done(((bf16[128,4,7168]{2,1,0:T(4,128)(2,1)}), bf16[128,4,7168]{2,1,0:T(4,128)(2,1)}, u32[]{:S(2)}, u32[]{:S(2)}) %all-to-all-start.1) | async-done | bytes 7340064 | tf_op jit(solution)/shard_map/all_to_all | solution.py:163
  494.4 6.8 %convert_reduce_fusion = f32[8,2,4,7168]{3,2,1,0:T(4,128)S(1)} fusion(bf16[128,4,7168]{2,1,0:T(4,128)(2,1)} %all-to-all-done.1), kind=kLoop, calls=%fused_computation.1 | loop fusion | flops 6881280 | bytes 9175040 | tf_op jit(solution)/shard_map/reduce_sum | solution.py:178
  501.2 2.7 fusion.8
  (38 shorter events, 0.2 us)
Async XLA Ops:
  7.2 328.8 %copy-start = (bf16[1,7168,128]{2,1,0:T(8,128)(2,1)S(1)}, bf16[1,7168,128]{2,1,0:T(8,128)(2,1)}, u32[]{:S(2)}) copy-start(bf16[1,7168,128]{2,1,0:T(8,128)(2,1)} %param.14) | copy-start | bytes 5505028
  7.2 117.4 %all-gather.5.cloned.1.call-start = ((), (), s32[]{:S(2)}) async-start(), calls=%async_computation.6 | async-start | bytes 3899392 | tf_op jit(solution)/shard_map/all_gather | solution.py:84
  36.5 250.1 %all-to-all-start = ((bf16[128,4,14337]{2,1,0:T(4,128)(2,1)}), bf16[128,4,14337]{2,1,0:T(4,128)(2,1)}, u32[]{:S(2)}, u32[]{:S(2)}) async-start(bf16[128,4,14337]{2,1,0:T(4,128)(2,1)} %pad_maximum_fusion), calls=%async_computation | async-start | bytes 29622272 | tf_op jit(solution)/shard_map/all_to_all | solution.py:25
  47.7 203.1 %all-gather.3.cloned.1.call-start = ((), (), s32[]{:S(2)}) async-start(), calls=%async_computation.5 | async-start | bytes 3899392 | tf_op jit(solution)/shard_map/all_gather | solution.py:85
  48.4 374.0 %reduce-scatter.4.cloned.1.call-start = ((), (), s32[]{:S(2)}) async-start(), calls=%async_computation.7 | async-start | bytes 6193152
  124.6 3.9 copy-start.3
  124.6 4.3 copy-start.6
  250.8 3.9 copy-start.4
  255.3 2.0 copy-start.8
  269.5 2.8 copy-start.7
  286.5 69.5 %all-to-all-start.2 = ((bf16[16,16,7168]{2,1,0:T(8,128)(2,1)}), bf16[16,16,7168]{2,1,0:T(8,128)(2,1)}, u32[]{:S(2)}, u32[]{:S(2)}) async-start(bf16[16,16,7168]{2,1,0:T(8,128)(2,1)} %bitcast.95), calls=%async_computation.2 | async-start | bytes 7340032 | tf_op jit(solution)/shard_map/all_to_all | solution.py:17
  336.0 5.8 %copy-start.1 = (bf16[512,7168]{1,0:T(8,128)(2,1)S(1)}, bf16[512,7168]{1,0:T(8,128)(2,1)}, u32[]{:S(2)}) copy-start(bf16[512,7168]{1,0:T(8,128)(2,1)} %reshape.93) | copy-start | bytes 22020100
  336.0 5.8 %copy-start.5 = (bf16[1,7168,128]{2,1,0:T(8,128)(2,1)S(1)}, bf16[1,7168,128]{2,1,0:T(8,128)(2,1)}, u32[]{:S(2)}) copy-start(bf16[1,7168,128]{2,1,0:T(8,128)(2,1)} %param.15) | copy-start | bytes 5505028
  341.8 3.1 copy-start.2
  341.8 3.6 copy-start.9
  356.0 38.8 %all-to-all-start.3 = ((bf16[128,1,4]{2,1,0:T(2,128)(2,1)}), bf16[128,1,4]{2,1,0:T(2,128)(2,1)S(1)}, u32[]{:S(2)}, u32[]{:S(2)}) async-start(bf16[128,1,4]{2,1,0:T(2,128)(2,1)} %convert_element_type.134), calls=%async_computation.3 | async-start | bytes 131072 | tf_op jit(solution)/shard_map/all_to_all | solution.py:170
  394.9 99.5 %all-to-all-start.1 = ((bf16[128,4,7168]{2,1,0:T(4,128)(2,1)}), bf16[128,4,7168]{2,1,0:T(4,128)(2,1)}, u32[]{:S(2)}, u32[]{:S(2)}) async-start(bf16[128,4,7168]{2,1,0:T(4,128)(2,1)} %reshape.94), calls=%async_computation.1 | async-start | bytes 14680064 | tf_op jit(solution)/shard_map/all_to_all | solution.py:163
  405.3 9.4 %slice-start = ((s8[7340032]{0:T(1024)(128)(4,1)}), s8[4194304]{0:T(1024)(128)(4,1)S(1)}, s32[]{:S(2)}) async-start(s8[7340032]{0:T(1024)(128)(4,1)} %bitcast.89), calls=%async_computation.8 | async-start | bytes 8388608
  408.0 6.6 %slice-start.1 = ((s8[7340032]{0:T(1024)(128)(4,1)}), s8[3145728]{0:T(1024)(128)(4,1)S(1)}, s32[]{:S(2)}) async-start(s8[7340032]{0:T(1024)(128)(4,1)} %bitcast.89), calls=%async_computation.9 | async-start | bytes 6291456
  408.0 10.0 %slice-start.2 = ((s8[7340032]{0:T(1024)(128)(4,1)}), s8[4194304]{0:T(1024)(128)(4,1)S(1)}, s32[]{:S(2)}) async-start(s8[7340032]{0:T(1024)(128)(4,1)} %bitcast.91), calls=%async_computation.10 | async-start | bytes 8388608
  414.7 3.4 slice-start.3
  418.0 3.6 copy-start.10
Sparse Core Ops, SparseCore 0:
  10.1 114.4 all-gather.4
  126.7 124.0 all-gather.2
  269.6 58.3 reduce-scatter.3
where the time goes:
time: 518 us; the launch traced here: 511 us
  waiting for transfers between devices  279 us (54%)
  local copies, waits for them, and re-layouts  78.7 us (15%)
  matrix products  64.5 us (12%)
  starting transfers between devices  46.4 us (9%)
  other arithmetic  27.8 us (5%)
  between operations  14.3 us (3%)
    all_gather x1, waiting for transfers between devices, shared_part(): lax.all_gather(grad_out, 'local', axis=0, tiled=True)  121 us
    all_gather x1, waiting for transfers between devices, shared_part(): lax.all_gather(tokens, 'local', axis=0, tiled=True)  75.6 us
    all_to_all x1, waiting for transfers between devices, routed_part(): lax.all_to_all(partial_value.reshape(got_in.shape), ('node', 'local'), sp...  70 us
    dot_general x4, matrix products, contract_last(): lax.dot_general(left, right, (((1,), (1,)), ((), ())), preferred_element_...  23.7 us
    dot_general x6, matrix products, contract_first(): lax.dot_general(left, right, (((0,), (0,)), ((), ())), preferred_element_...  15.5 us
    all_to_all x1, starting transfers between devices, routed_part(): lax.all_to_all(score.reshape(got_gate.shape), ('node', 'local'), split_ax...  15.4 us
    slice x1, local copies, waits for them, and re-layouts, in_one_piece(): piece = out[..., at:at + column.shape[along]]  15.1 us
    reshape x1, local copies, waits for them, and re-layouts, routed_part(): partial_value.reshape(got_in.shape)  12.7 us
  transfers between devices with their start and end apart: 7, of which 4 were waited for; matrix products, arithmetic and copies ran while one was open for 31% of the time, Pallas kernels for 0%

commit v1 on v0

--- a/solution.py
+++ b/solution.py
@@ -5,6 +5,28 @@
 
 E_NODE = 2
 precise = lax.Precision.HIGHEST
+
+
+def joined_along(tiles, dim):
+    lengths = list(tiles.shape[1:])
+    lengths[dim] *= tiles.shape[0]
+    return jnp.moveaxis(tiles, 0, dim).reshape(lengths)
+
+
+def gather_around(x, axis, dim):
+    size = lax.axis_size(axis)
+    pairs = [(i, (i + 1) % size) for i in range(size)]
+    back = [(b, a) for a, b in pairs]
+    lower, upper = ([], [])
+    for step in range(size - 1):
+        if step % 2 == 0:
+            lower.append(lax.ppermute(lower[-1] if lower else x, axis, pairs))
+        else:
+            upper.append(lax.ppermute(upper[-1] if upper else x, axis, back))
+    tiles = jnp.stack([*lower[::-1], x, *upper])
+    shift = lax.axis_index(axis) - len(lower)
+    tiles = tiles[(jnp.arange(size) - shift) % size]
+    return joined_along(tiles, dim)
 
 
 def split_up(value, dim, devices):
@@ -81,7 +103,7 @@
 
 def shared_part(tokens, grad_out, s_gate, s_up, s_down):
     rows_in, rows_grad = (
-        lax.all_gather(tokens, "local", axis=0, tiled=True),
+        gather_around(tokens, "local", 0),
         lax.all_gather(grad_out, "local", axis=0, tiled=True),
     )
     unit_weight = jnp.ones((rows_in.shape[0], 1), jnp.float32)

time: 518 us -> 591 us (1.14)
  starting transfers between devices: 46.4 us -> 105 us
  local copies, waits for them, and re-layouts: 78.7 us -> 101 us
  waiting for transfers between devices: 279 us -> 270 us
    ppermute x0 -> x15, waiting for transfers between devices: none -> 200 us  [the longest x7 178 us: gather_around(): upper.append(lax.ppermute(upper[-1] if upper else x, axis, back))]
    all_gather x1, waiting for transfers between devices: 121 us -> 0.02 us  [shared_part(): lax.all_gather(grad_out, 'local', axis=0, tiled=True)]
    all_gather x1 -> x0, waiting for transfers between devices: 75.6 us -> none  [shared_part(): lax.all_gather(tokens, 'local', axis=0, tiled=True)]
    all_to_all x1, starting transfers between devices: 11.2 us -> 35.4 us  [in_one_piece(): lax.all_to_all(both, axis, split_axis=split_dim, concat_axis=concat_dim,...]
    ppermute x0 -> x15, starting transfers between devices: none -> 22.1 us  [the longest x7 19.4 us: gather_around(): upper.append(lax.ppermute(upper[-1] if upper else x, axis, back))]
    all_to_all x1, starting transfers between devices: 8.77 us -> 26 us  [summed_on_arrival(): lax.all_to_all(tiles, axis, split_axis=0, concat_axis=0, tiled=True)]
    unnamed x32 -> x55, local copies, waits for them, and re-layouts: 11.2 us -> 28.3 us
    all_to_all x1, waiting for transfers between devices: 11.3 us -> 0.01 us  [in_one_piece(): lax.all_to_all(both, axis, split_axis=split_dim, concat_axis=concat_dim,...]
  transfers between devices with their start and end apart: 7 -> 21, of which waited for: 4 -> 10; matrix products, arithmetic and copies ran while one was open for 31% -> 31% of each run, Pallas kernels for 0% -> 0%
where the time goes in v1:
time: 591 us; the launch traced here: 583 us
  waiting for transfers between devices  270 us (46%)
  starting transfers between devices  105 us (18%)
  local copies, waits for them, and re-layouts  101 us (17%)
  matrix products  64.6 us (11%)
  other arithmetic  27.8 us (5%)
  between operations  14.7 us (2%)
    ppermute x7, waiting for transfers between devices, gather_around(): upper.append(lax.ppermute(upper[-1] if upper else x, axis, back))  178 us
    all_to_all x1, waiting for transfers between devices, routed_part(): lax.all_to_all(partial_value.reshape(got_in.shape), ('node', 'local'), sp...  70 us
    all_to_all x1, starting transfers between devices, in_one_piece(): lax.all_to_all(both, axis, split_axis=split_dim, concat_axis=concat_dim,...  35.4 us
    unnamed x55, local copies, waits for them, and re-layouts  28.3 us
    all_to_all x1, starting transfers between devices, summed_on_arrival(): lax.all_to_all(tiles, axis, split_axis=0, concat_axis=0, tiled=True)  26 us
    dot_general x4, matrix products, contract_last(): lax.dot_general(left, right, (((1,), (1,)), ((), ())), preferred_element_...  23.8 us
    ppermute x8, waiting for transfers between devices, gather_around(): lower.append(lax.ppermute(lower[-1] if lower else x, axis, pairs))  22.5 us
    ppermute x7, starting transfers between devices, gather_around(): upper.append(lax.ppermute(upper[-1] if upper else x, axis, back))  19.4 us
  transfers between devices with their start and end apart: 21, of which 10 were waited for; matrix products, arithmetic and copies ran while one was open for 31% of the time, Pallas kernels for 0%

profile of v1, /device:TPU:11, one launch (start us, length us, event | category | flops | bytes accessed | tf_op | source)
XLA Modules:
  0.0 583.2 jit_solution(12146316255756262873)
XLA Ops:
  7.2 1.3 collective-permute-start
  8.5 5.5 collective-permute-done
  14.0 1.2 collective-permute-start.1
  15.2 1.2 collective-permute-start.8
  16.4 4.4 collective-permute-done.1
  20.9 3.3 collective-permute-start.9
  24.2 3.6 collective-permute-done.2
  27.8 0.8 fusion.29
  28.6 3.3 collective-permute-start.10
  32.0 2.6 collective-permute-done.3
  35.3 0.8 select_reduce_fusion.3
  36.7 3.6 collective-permute-start.11
  40.4 1.5 collective-permute-done.4
  41.9 1.4 convolution_convert_fusion.6
  44.0 0.9 collective-permute-done.11
  44.9 4.0 collective-permute-start.12
  48.9 2.9 collective-permute-done.5
  51.8 1.5 convolution_convert_fusion.7
  54.0 3.4 collective-permute-start.13
  57.4 1.9 collective-permute-done.6
  59.5 5.2 broadcast_in_dim.61
  64.7 5.2 broadcast_in_dim.63
  69.9 11.0 %pad_maximum_fusion = bf16[128,4,14337]{2,1,0:T(4,128)(2,1)} fusion(bf16[128,4,1]{2,1,0:T(4,128)(2,1)S(1)} %copy.67, bf16[128,4,7168]{2,1,0:T(4,128)(2,1)} %bitcast.129, bf16[128,4,7168]{2,1,0:T(4,128)(2,1)} %bitcast.128), kind=kLoop, calls=%fused_computation.1 | loop fusion | flops 44043264 | bytes 29362176 | tf_op jit(solution)/shard_map/concatenate | solution.py:45
  80.9 35.4 %all-to-all-start = ((bf16[128,4,14337]{2,1,0:T(4,128)(2,1)}), bf16[128,4,14337]{2,1,0:T(4,128)(2,1)}, u32[]{:S(2)}, u32[]{:S(2)}) async-start(bf16[128,4,14337]{2,1,0:T(4,128)(2,1)} %pad_maximum_fusion), calls=%async_computation | async-start | bytes 29622272 | tf_op jit(solution)/shard_map/all_to_all | solution.py:47
  117.0 1.6 bitcast_dynamic-update-slice_fusion.15
  118.6 1.6 bitcast_dynamic-update-slice_fusion.14
  120.3 1.6 bitcast_dynamic-update-slice_fusion.13
  121.9 1.7 bitcast_dynamic-update-slice_fusion.12
  123.6 1.6 bitcast_dynamic-update-slice_fusion.11
  130.9 1.6 bitcast_dynamic-update-slice_fusion.2
  132.5 1.6 bitcast_dynamic-update-slice_fusion.1
  134.1 176.9 %collective-permute-done.14 = bf16[16,7168]{1,0:T(8,128)(2,1)S(1)} collective-permute-done((bf16[16,7168]{1,0:T(8,128)(2,1)}, bf16[16,7168]{1,0:T(8,128)(2,1)S(1)}, u32[]{:S(2)}, u32[]{:S(2)}) %collective-permute-start.14) | collective-permute-done | bytes 229408 | tf_op jit(solution)/shard_map/ppermute | solution.py:25
  311.7 4.6 gather_fusion
  316.3 3.9 fusion.44
  320.6 1.2 fusion.43
  321.8 3.9 multiply_convert_fusion.5
  327.1 1.3 copy-done.8
  329.1 3.0 pad_maximum_fusion.1
  332.2 8.3 %copy.90 = bf16[7168,384]{1,0:T(8,128)(2,1)} copy(bf16[7168,384]{0,1:T(8,128)(2,1)} %pad_maximum_fusion.1) | data formatting | bytes 11010048
  340.5 2.7 fusion.45
  343.2 2.9 fusion
  346.2 26.0 %all-to-all-start.2 = ((bf16[16,16,7168]{2,1,0:T(8,128)(2,1)}), bf16[16,16,7168]{2,1,0:T(8,128)(2,1)}, u32[]{:S(2)}, u32[]{:S(2)}) async-start(bf16[16,16,7168]{2,1,0:T(8,128)(2,1)} %bitcast.130), calls=%async_computation.2 | async-start | bytes 7340032 | tf_op jit(solution)/shard_map/all_to_all | solution.py:39
  372.2 15.2 %fusion.41 = (bf16[128,4,7168]{2,1,0:T(4,128)(2,1)}, bf16[128,4,7168]{2,1,0:T(4,128)(2,1)}) fusion(bf16[128,4,14337]{2,1,0:T(4,128)(2,1)} %all-to-all-done), kind=kLoop, calls=%fused_computation.90 | loop fusion | bytes 29360128 | tf_op jit(solution)/shard_map/slice | solution.py:52
  387.4 1.1 convert_reduce_fusion.2
  388.6 12.2 %reshape.144 = bf16[512,7168]{1,0:T(8,128)(2,1)} reshape(bf16[128,4,7168]{2,1,0:T(4,128)(2,1)} %get-tuple-element.48) | data formatting | bytes 14680064 | tf_op jit(solution)/shard_map/reshape | solution.py:178
  400.8 12.1 %reshape.145 = bf16[512,7168]{1,0:T(8,128)(2,1)} reshape(bf16[128,4,7168]{2,1,0:T(4,128)(2,1)} %get-tuple-element.49) | data formatting | bytes 14680064 | tf_op jit(solution)/shard_map/reshape | solution.py:177
  412.9 5.8 fusion.9
  418.7 2.5 fusion.12
  422.3 2.6 multiply_reduce_fusion
  424.9 0.8 convert_element_type.134
  425.7 7.3 %fusion.7 = f32[512,7168]{1,0:T(8,128)} fusion(bf16[512,128]{0,1:T(8,128)(2,1)S(1)} %get-tuple-element.51, bf16[1,7168,128]{2,1,0:T(8,128)(2,1)S(1)} %copy-done), kind=kOutput, calls=%fused_computation.23 | convolution fusion | flops 939524096 | bytes 16646144 | tf_op jit(solution)/shard_map/dot_general | solution.py:70
  433.0 10.7 %all-to-all-start.3 = ((bf16[128,1,4]{2,1,0:T(2,128)(2,1)}), bf16[128,1,4]{2,1,0:T(2,128)(2,1)S(1)}, u32[]{:S(2)}, u32[]{:S(2)}) async-start(bf16[128,1,4]{2,1,0:T(2,128)(2,1)} %convert_element_type.134), calls=%async_computation.3 | async-start | bytes 131072 | tf_op jit(solution)/shard_map/all_to_all | solution.py:192
  443.7 10.8 %add_convert_fusion = bf16[512,7168]{1,0:T(8,128)(2,1)} fusion(f32[512,7168]{1,0:T(8,128)} %fusion.7, bf16[512,128]{0,1:T(8,128)(2,1)S(1)} %get-tuple-element.55, bf16[1,7168,128]{2,1,0:T(8,128)(2,1)} %param.15), kind=kOutput, calls=%fused_computation.3 | convolution fusion | flops 946864128 | bytes 23986176 | tf_op jit(solution)/shard_map/dot_general | solution.py:70
  454.5 12.6 %reshape.146 = bf16[128,4,7168]{2,1,0:T(4,128)(2,1)} reshape(bf16[512,7168]{1,0:T(8,128)(2,1)} %add_convert_fusion) | data formatting | bytes 14680064 | tf_op jit(solution)/shard_map/reshape | solution.py:186
  467.1 10.3 %all-to-all-start.1 = ((bf16[128,4,7168]{2,1,0:T(4,128)(2,1)}), bf16[128,4,7168]{2,1,0:T(4,128)(2,1)}, u32[]{:S(2)}, u32[]{:S(2)}) async-start(bf16[128,4,7168]{2,1,0:T(4,128)(2,1)} %reshape.146), calls=%async_computation.1 | async-start | bytes 14680064 | tf_op jit(solution)/shard_map/all_to_all | solution.py:185
  477.5 2.7 convert_reduce_fusion.1
  480.2 6.6 %fusion.1 = bf16[1,7168,128]{2,1,0:T(8,128)(2,1)} fusion(bf16[512,7168]{1,0:T(8,128)(2,1)} %reshape.145, bf16[512,128]{0,1:T(8,128)(2,1)S(1)} %get-tuple-element.51), kind=kOutput, calls=%fused_computation.12 | convolution fusion | flops 940441600 | bytes 9306112 | tf_op jit(solution)/shard_map/dot_general | solution.py:64
  486.9 3.4 fusion.2
  490.2 3.4 fusion.3
  493.9 0.7 select_reduce_fusion.2
  494.6 2.0 fusion.42
  496.6 70.0 %all-to-all-done.1 = bf16[128,4,7168]{2,1,0:T(4,128)(2,1)} async-done(((bf16[128,4,7168]{2,1,0:T(4,128)(2,1)}), bf16[128,4,7168]{2,1,0:T(4,128)(2,1)}, u32[]{:S(2)}, u32[]{:S(2)}) %all-to-all-start.1) | async-done | bytes 7340064 | tf_op jit(solution)/shard_map/all_to_all | solution.py:185
  566.6 6.8 %convert_reduce_fusion = f32[8,2,4,7168]{3,2,1,0:T(4,128)S(1)} fusion(bf16[128,4,7168]{2,1,0:T(4,128)(2,1)} %all-to-all-done.1), kind=kLoop, calls=%fused_computation.2 | loop fusion | flops 6881280 | bytes 9175040 | tf_op jit(solution)/shard_map/reduce_sum | solution.py:200
  573.4 2.7 fusion.6
  (92 shorter events, 14.0 us)
Async XLA Ops:
  7.2 405.7 %copy-start = (bf16[1,7168,128]{2,1,0:T(8,128)(2,1)S(1)}, bf16[1,7168,128]{2,1,0:T(8,128)(2,1)}, u32[]{:S(2)}) copy-start(bf16[1,7168,128]{2,1,0:T(8,128)(2,1)} %param.14) | copy-start | bytes 5505028
  7.2 314.6 %all-gather.2.cloned.1.call-start = ((), (), s32[]{:S(2)}) async-start(), calls=%async_computation.5 | async-start | bytes 3899392 | tf_op jit(solution)/shard_map/all_gather | solution.py:107
  7.2 6.8 %collective-permute-start = (bf16[16,7168]{1,0:T(8,128)(2,1)}, bf16[16,7168]{1,0:T(8,128)(2,1)S(1)}, u32[]{:S(2)}, u32[]{:S(2)}) collective-permute-start(bf16[16,7168]{1,0:T(8,128)(2,1)} %param.10), channel_id=1, source_target_pairs={{0,1},{1,2},{2,3},{3,4},{4,5},{5,6},{6,7},{7,8},{8,9},{9,10},{10,1... | collective-permute-start | bytes 688136 | tf_op jit(solution)/shard_map/ppermute | solution.py:23
  14.0 6.8 %collective-permute-start.1 = (bf16[16,7168]{1,0:T(8,128)(2,1)S(1)}, bf16[16,7168]{1,0:T(8,128)(2,1)S(1)}, u32[]{:S(2)}, u32[]{:S(2)}) collective-permute-start(bf16[16,7168]{1,0:T(8,128)(2,1)S(1)} %collective-permute-done), channel_id=1, source_target_pairs={{0,1},{1,2},{2,3},{3,4},{4,5},{5,6},{6,7},{7,8},{8,9},{9,10},{10,1... | collective-permute-start | bytes 688136 | tf_op jit(solution)/shard_map/ppermute | solution.py:23
  15.2 5.7 collective-permute-start.8
  20.8 7.0 %collective-permute-start.2 = (bf16[16,7168]{1,0:T(8,128)(2,1)S(1)}, bf16[16,7168]{1,0:T(8,128)(2,1)S(1)}, u32[]{:S(2)}, u32[]{:S(2)}) collective-permute-start(bf16[16,7168]{1,0:T(8,128)(2,1)S(1)} %collective-permute-done.1), channel_id=1, source_target_pairs={{0,1},{1,2},{2,3},{3,4},{4,5},{5,6},{6,7},{7,8},{8,9},{9,10},{10,1... | collective-permute-start | bytes 688136 | tf_op jit(solution)/shard_map/ppermute | solution.py:23
  20.9 7.7 %collective-permute-start.9 = (bf16[16,7168]{1,0:T(8,128)(2,1)S(1)}, bf16[16,7168]{1,0:T(8,128)(2,1)S(1)}, u32[]{:S(2)}, u32[]{:S(2)}) collective-permute-start(bf16[16,7168]{1,0:T(8,128)(2,1)S(1)} %collective-permute-done.8), channel_id=1, source_target_pairs={{1,0},{2,1},{3,2},{4,3},{5,4},{6,5},{7,6},{8,7},{9,8},{10,9},{11,1... | collective-permute-start | bytes 688136 | tf_op jit(solution)/shard_map/ppermute | solution.py:25
  27.8 6.8 %collective-permute-start.3 = (bf16[16,7168]{1,0:T(8,128)(2,1)S(1)}, bf16[16,7168]{1,0:T(8,128)(2,1)}, u32[]{:S(2)}, u32[]{:S(2)}) collective-permute-start(bf16[16,7168]{1,0:T(8,128)(2,1)S(1)} %collective-permute-done.2), channel_id=1, source_target_pairs={{0,1},{1,2},{2,3},{3,4},{4,5},{5,6},{6,7},{7,8},{8,9},{9,10},{10,1... | collective-permute-start | bytes 688136 | tf_op jit(solution)/shard_map/ppermute | solution.py:23
  28.6 8.1 %collective-permute-start.10 = (bf16[16,7168]{1,0:T(8,128)(2,1)S(1)}, bf16[16,7168]{1,0:T(8,128)(2,1)S(1)}, u32[]{:S(2)}, u32[]{:S(2)}) collective-permute-start(bf16[16,7168]{1,0:T(8,128)(2,1)S(1)} %collective-permute-done.9), channel_id=1, source_target_pairs={{1,0},{2,1},{3,2},{4,3},{5,4},{6,5},{7,6},{8,7},{9,8},{10,9},{11,1... | collective-permute-start | bytes 688136 | tf_op jit(solution)/shard_map/ppermute | solution.py:25
  34.6 7.3 %collective-permute-start.4 = (bf16[16,7168]{1,0:T(8,128)(2,1)}, bf16[16,7168]{1,0:T(8,128)(2,1)}, u32[]{:S(2)}, u32[]{:S(2)}) collective-permute-start(bf16[16,7168]{1,0:T(8,128)(2,1)} %collective-permute-done.3), channel_id=1, source_target_pairs={{0,1},{1,2},{2,3},{3,4},{4,5},{5,6},{6,7},{7,8},{8,9},{9,10},{10,1... | collective-permute-start | bytes 688136 | tf_op jit(solution)/shard_map/ppermute | solution.py:23
  36.7 8.1 %collective-permute-start.11 = (bf16[16,7168]{1,0:T(8,128)(2,1)S(1)}, bf16[16,7168]{1,0:T(8,128)(2,1)S(1)}, u32[]{:S(2)}, u32[]{:S(2)}) collective-permute-start(bf16[16,7168]{1,0:T(8,128)(2,1)S(1)} %collective-permute-done.10), channel_id=1, source_target_pairs={{1,0},{2,1},{3,2},{4,3},{5,4},{6,5},{7,6},{8,7},{9,8},{10,9},{11,1... | collective-permute-start | bytes 688136 | tf_op jit(solution)/shard_map/ppermute | solution.py:25
  41.9 9.9 %collective-permute-start.5 = (bf16[16,7168]{1,0:T(8,128)(2,1)}, bf16[16,7168]{1,0:T(8,128)(2,1)S(1)}, u32[]{:S(2)}, u32[]{:S(2)}) collective-permute-start(bf16[16,7168]{1,0:T(8,128)(2,1)} %collective-permute-done.4), channel_id=1, source_target_pairs={{0,1},{1,2},{2,3},{3,4},{4,5},{5,6},{6,7},{7,8},{8,9},{9,10},{10,1... | collective-permute-start | bytes 688136 | tf_op jit(solution)/shard_map/ppermute | solution.py:23
  44.9 19.8 %copy-start.11 = (bf16[16,7168]{1,0:T(8,128)(2,1)}, bf16[16,7168]{1,0:T(8,128)(2,1)S(1)}, u32[]{:S(2)}) copy-start(bf16[16,7168]{1,0:T(8,128)(2,1)S(1)} %collective-permute-done.11) | copy-start | bytes 688132
  44.9 9.1 %collective-permute-start.12 = (bf16[16,7168]{1,0:T(8,128)(2,1)S(1)}, bf16[16,7168]{1,0:T(8,128)(2,1)}, u32[]{:S(2)}, u32[]{:S(2)}) collective-permute-start(bf16[16,7168]{1,0:T(8,128)(2,1)S(1)} %collective-permute-done.11), channel_id=1, source_target_pairs={{1,0},{2,1},{3,2},{4,3},{5,4},{6,5},{7,6},{8,7},{9,8},{10,9},{11,1... | collective-permute-start | bytes 688136 | tf_op jit(solution)/shard_map/ppermute | solution.py:25
  51.8 12.9 %copy-start.13 = (bf16[16,7168]{1,0:T(8,128)(2,1)}, bf16[16,7168]{1,0:T(8,128)(2,1)S(1)}, u32[]{:S(2)}) copy-start(bf16[16,7168]{1,0:T(8,128)(2,1)S(1)} %collective-permute-done.5) | copy-start | bytes 688132
  51.8 7.5 %collective-permute-start.6 = (bf16[16,7168]{1,0:T(8,128)(2,1)S(1)}, bf16[16,7168]{1,0:T(8,128)(2,1)}, u32[]{:S(2)}, u32[]{:S(2)}) collective-permute-start(bf16[16,7168]{1,0:T(8,128)(2,1)S(1)} %collective-permute-done.5), channel_id=1, source_target_pairs={{0,1},{1,2},{2,3},{3,4},{4,5},{5,6},{6,7},{7,8},{8,9},{9,10},{10,1... | collective-permute-start | bytes 688136 | tf_op jit(solution)/shard_map/ppermute | solution.py:23
  54.0 62.4 %collective-permute-start.13 = (bf16[16,7168]{1,0:T(8,128)(2,1)}, bf16[16,7168]{1,0:T(8,128)(2,1)}, u32[]{:S(2)}, u32[]{:S(2)}) collective-permute-start(bf16[16,7168]{1,0:T(8,128)(2,1)} %collective-permute-done.12), channel_id=1, source_target_pairs={{1,0},{2,1},{3,2},{4,3},{5,4},{6,5},{7,6},{8,7},{9,8},{10,9},{11,1... | collective-permute-start | bytes 688136 | tf_op jit(solution)/shard_map/ppermute | solution.py:25
  59.3 57.7 %collective-permute-start.7 = (bf16[16,7168]{1,0:T(8,128)(2,1)}, bf16[16,7168]{1,0:T(8,128)(2,1)}, u32[]{:S(2)}, u32[]{:S(2)}) collective-permute-start(bf16[16,7168]{1,0:T(8,128)(2,1)} %collective-permute-done.6), channel_id=1, source_target_pairs={{0,1},{1,2},{2,3},{3,4},{4,5},{5,6},{6,7},{7,8},{8,9},{9,10},{10,1... | collective-permute-start | bytes 688136 | tf_op jit(solution)/shard_map/ppermute | solution.py:23
  80.9 265.3 %all-to-all-start = ((bf16[128,4,14337]{2,1,0:T(4,128)(2,1)}), bf16[128,4,14337]{2,1,0:T(4,128)(2,1)}, u32[]{:S(2)}, u32[]{:S(2)}) async-start(bf16[128,4,14337]{2,1,0:T(4,128)(2,1)} %pad_maximum_fusion), calls=%async_computation | async-start | bytes 29622272 | tf_op jit(solution)/shard_map/all_to_all | solution.py:47
  116.3 11.0 %copy-start.10 = (bf16[16,7168]{1,0:T(8,128)(2,1)S(1)}, bf16[16,7168]{1,0:T(8,128)(2,1)}, u32[]{:S(2)}) copy-start(bf16[16,7168]{1,0:T(8,128)(2,1)} %param.10) | copy-start | bytes 688132
  116.3 378.3 %reduce-scatter.4.cloned.1.call-start = ((), (), s32[]{:S(2)}) async-start(), calls=%async_computation.6 | async-start | bytes 6193152
  116.4 13.8 %copy-start.12 = (bf16[16,7168]{1,0:T(8,128)(2,1)S(1)}, bf16[16,7168]{1,0:T(8,128)(2,1)}, u32[]{:S(2)}) copy-start(bf16[16,7168]{1,0:T(8,128)(2,1)} %copy-done.11) | copy-start | bytes 688132
  116.4 194.6 %collective-permute-start.14 = (bf16[16,7168]{1,0:T(8,128)(2,1)}, bf16[16,7168]{1,0:T(8,128)(2,1)S(1)}, u32[]{:S(2)}, u32[]{:S(2)}) collective-permute-start(bf16[16,7168]{1,0:T(8,128)(2,1)} %collective-permute-done.13), channel_id=1, source_target_pairs={{1,0},{2,1},{3,2},{4,3},{5,4},{6,5},{7,6},{8,7},{9,8},{10,9},{11,1... | collective-permute-start | bytes 688136 | tf_op jit(solution)/shard_map/ppermute | solution.py:25
  316.3 3.9 copy-start.2
  316.3 4.3 copy-start.6
  321.8 3.9 copy-start.3
  326.4 2.0 copy-start.8
  340.5 2.8 copy-start.7
  346.2 86.8 %all-to-all-start.2 = ((bf16[16,16,7168]{2,1,0:T(8,128)(2,1)}), bf16[16,16,7168]{2,1,0:T(8,128)(2,1)}, u32[]{:S(2)}, u32[]{:S(2)}) async-start(bf16[16,16,7168]{2,1,0:T(8,128)(2,1)} %bitcast.130), calls=%async_computation.2 | async-start | bytes 7340032 | tf_op jit(solution)/shard_map/all_to_all | solution.py:39
  412.9 5.8 copy-start.1
  412.9 5.8 copy-start.5
  418.7 3.1 copy-start.4
  418.7 3.6 copy-start.9
  433.0 34.1 %all-to-all-start.3 = ((bf16[128,1,4]{2,1,0:T(2,128)(2,1)}), bf16[128,1,4]{2,1,0:T(2,128)(2,1)S(1)}, u32[]{:S(2)}, u32[]{:S(2)}) async-start(bf16[128,1,4]{2,1,0:T(2,128)(2,1)} %convert_element_type.134), calls=%async_computation.3 | async-start | bytes 131072 | tf_op jit(solution)/shard_map/all_to_all | solution.py:192
  467.1 99.5 %all-to-all-start.1 = ((bf16[128,4,7168]{2,1,0:T(4,128)(2,1)}), bf16[128,4,7168]{2,1,0:T(4,128)(2,1)}, u32[]{:S(2)}, u32[]{:S(2)}) async-start(bf16[128,4,7168]{2,1,0:T(4,128)(2,1)} %reshape.146), calls=%async_computation.1 | async-start | bytes 14680064 | tf_op jit(solution)/shard_map/all_to_all | solution.py:185
  477.5 9.4 %slice-start = ((s8[7340032]{0:T(1024)(128)(4,1)}), s8[4194304]{0:T(1024)(128)(4,1)S(1)}, s32[]{:S(2)}) async-start(s8[7340032]{0:T(1024)(128)(4,1)} %bitcast.120), calls=%async_computation.7 | async-start | bytes 8388608
  480.2 6.6 %slice-start.1 = ((s8[7340032]{0:T(1024)(128)(4,1)}), s8[3145728]{0:T(1024)(128)(4,1)S(1)}, s32[]{:S(2)}) async-start(s8[7340032]{0:T(1024)(128)(4,1)} %bitcast.120), calls=%async_computation.8 | async-start | bytes 6291456
  480.2 10.0 %slice-start.2 = ((s8[7340032]{0:T(1024)(128)(4,1)}), s8[4194304]{0:T(1024)(128)(4,1)S(1)}, s32[]{:S(2)}) async-start(s8[7340032]{0:T(1024)(128)(4,1)} %bitcast.126), calls=%async_computation.9 | async-start | bytes 8388608
  486.9 3.4 slice-start.3
  490.2 3.6 copy-start.14
Sparse Core Ops, SparseCore 0:
  21.0 65.7 all-gather.1
  340.6 59.4 reduce-scatter.3
